TPU v7x, 32 devices: a whole 2x2x4 slice. The times are simulated.
32 devices in a mesh: row: 16 (over z, x, core), col: 2 (over y).
Axes of the slice: x: 2, y: 2, z: 4, core: 2. Of those that a mesh axis runs over, the one named last changes fastest.
Arguments:
- activations: bfloat16 [128, 16384], P('col', 'row'), may hold values from 0 to 2
- blocks_one: bfloat16 [16, 2, 64, 128, 128], P('row', 'col'), may hold values from -0.25 to 0.25
- pattern_one: int32 [16, 2, 64], P('row', 'col'), may hold values from 0 to 511, as said below
- count_one: int32 [16, 2], P('row', 'col'), may hold values from 1 to 64, as said below
- blocks_two: bfloat16 [2, 16, 64, 128, 128], P('col', 'row'), may hold values from -0.375 to 0.375
- pattern_two: int32 [2, 16, 64], P('col', 'row'), may hold values from 0 to 511, as said below
- count_two: int32 [2, 16], P('col', 'row'), may hold values from 1 to 64, as said below
Outputs:
- sparse_out: bfloat16 [128, 16384], P('col', 'row')
Inputs may be any that keep to these rules, and one draw needn't show every extreme that they name: `pattern_one`: in each tile the slots below its count hold distinct positions; slots at or above the count hold positions in range whose blocks are not part of the weights. `count_one`: some tile has exactly 64 live slots. `pattern_two`: in each tile the slots below its count hold distinct positions; slots at or above the count hold positions in range whose blocks are not part of the weights. `count_two`: some tile has exactly 64 live slots.
All inputs are finite; a program needn't handle non-finite values.
Results may differ from a plain program's by a relative error of at most 0.0053.
Values may be sent and summed in bfloat16 or wider, within the bound.
No kernel may reach another device: no remote copies, remote signals or barrier semaphores. Data moves between devices by JAX's collectives and lax.ppermute only.
A program may use at most 64 MiB of HBM per device.

v0:
```python
import functools

import jax
import jax.numpy as jnp
from jax import lax
from jax.experimental import pallas as pl
from jax.experimental.pallas import tpu as pltpu
from jax.sharding import PartitionSpec as P


bias_value = -0.3
CORES = 2
DEPTH = 4
UNROLL = 8
SEND = jnp.float32
SPARE = 1024 * 1024


def split(value, by):
    if by & (by - 1) == 0:
        return lax.shift_right_logical(value, by.bit_length() - 1), value & (by - 1)
    return value // by, value % by


def turned(digit, by, size):
    if size & (size - 1) == 0:
        return digit ^ by
    return (digit + by) % size


def behind(here, there, size):
    if size & (size - 1) == 0:
        return here ^ there
    return (here - there + size) % size


def digit_shift(sizes, which, by):
    total = sizes[0] * sizes[1] * sizes[2]
    stride = 1
    for size in sizes[which + 1 :]:
        stride *= size
    size = sizes[which]
    pairs = []
    for r in range(total):
        d = (r // stride) % size
        pairs.append((r, r + (turned(d, by, size) - d) * stride))
    return pairs


def first_kernel(sizes, groups, load, pattern, count, act, blocks, *refs):
    _, _, cores = sizes
    _, size, _ = blocks.shape
    if load:
        send, keep, held, stage, acc, sems = refs
        copies = [
            pltpu.make_async_copy(act.at[:, pl.ds(r * size, size)], stage.at[r], sems.at[r])
            for r in range(stage.shape[0])
        ]
        copies.append(pltpu.make_async_copy(blocks, held, sems.at[stage.shape[0]]))
        for copy in copies:
            copy.start()
        blocks = held
    else:
        send, keep, stage, acc = refs
    units, m, _ = acc.shape
    units -= groups
    columns = units // groups
    live = count[0, 0]
    if not load:
        for r in range(stage.shape[0]):
            stage[r] = act[:, r * size : (r + 1) * size]

    def clear(u, _):
        acc[u] = jnp.zeros((m, size), jnp.float32)
        return 0

    lax.fori_loop(0, units, clear, 0, unroll=8)
    if load:
        for copy in copies:
            copy.wait()

    def step(t, _):
        base = t * UNROLL
        found = []
        for j in range(UNROLL):
            r, c = split(pattern[0, base + j], columns)
            product = jnp.dot(stage[r], blocks[base + j], preferred_element_type=jnp.float32)
            found.append((c, product))
        for j, (c, product) in enumerate(found):
            used = base + j < live
            for g in range(groups):
                at = jnp.where(used, g * columns + c, units + g)
                acc[at] += product[g * m : (g + 1) * m]
        return 0

    lax.fori_loop(0, (live + UNROLL - 1) // UNROLL, step, 0)
    core = lax.axis_index("row") % cores
    half = units // cores
    mine = core * half
    other = (cores - 1 - core) * half

    def leave(u, _):
        send[u] = acc[other + u].astype(send.dtype)
        keep[u] = acc[mine + u]
        return 0

    lax.fori_loop(0, half, leave, 0, unroll=4)


def spread_kernel(sizes, which, *refs):
    size = sizes[which]
    arrays, outs = refs[:-size], refs[-size:]
    stride = 1
    for s in sizes[which + 1 :]:
        stride *= s
    here = lax.axis_index("row") // stride % size

    def step(j, _):
        for k, out in enumerate(outs):
            at = turned(here, k, size)
            total = arrays[0][at, j]
            for a in arrays[1:]:
                total = total + a[at, j].astype(jnp.float32)
            out[j] = total.astype(out.dtype)
        return 0

    lax.fori_loop(0, outs[0].shape[0], step, 0, unroll=2)


def finish_kernel(*refs):
    def step(j, _):
        total = refs[0][j]
        for a in refs[1:-1]:
            total = total + a[j].astype(jnp.float32)
        refs[-1][j] = jnp.maximum(total + bias_value, 0.0).astype(jnp.bfloat16)
        return 0

    lax.fori_loop(0, refs[0].shape[0], step, 0, unroll=True if refs[0].shape[0] < 8 else 4)


def join_kernel(*refs):
    n = refs[0].shape[0]
    for i, ref in enumerate(refs[:-1]):
        for j in range(n):
            refs[-1][i * n + j] = ref[j]


def second_kernel(sizes, groups, pattern, count, *refs):
    depth, width, cores = sizes
    pieces = refs[: width * cores]
    blocks, out, acc = refs[width * cores :]
    _, size, _ = blocks.shape
    per, m, _ = pieces[0].shape
    columns = acc.shape[0] - 1
    rows_in = per * width * cores // groups
    each = per // depth
    live = count[0, 0]
    row = lax.axis_index("row")
    core, x, z = row % cores, row // cores % width, row // (cores * width)
    for c in range(columns):
        acc[c] = jnp.zeros(acc.shape[1:], jnp.float32)

    def hidden(u):
        rest, j = split(u, each)
        rest, zd = split(rest, depth)
        cd, xd = split(rest, width)
        piece = behind(core, cd, cores) * width + behind(x, xd, width)
        at = behind(z, zd, depth) * each + j
        found = pieces[0][at]
        for i in range(1, len(pieces)):
            found = jnp.where(piece == i, pieces[i][at], found)
        return found

    def step(t, _):
        base = t * UNROLL
        found = []
        for j in range(UNROLL):
            block = blocks[base + j]
            r, c = split(pattern[0, base + j], columns)
            products = [
                jnp.dot(hidden(g * rows_in + r), block, preferred_element_type=jnp.float32) for g in range(groups)
            ]
            found.append((c, products))
        for j, (c, products) in enumerate(found):
            at = jnp.where(base + j < live, c, columns)
            for g, product in enumerate(products):
                acc[at, g * m : (g + 1) * m] += product
        return 0

    lax.fori_loop(0, (live + UNROLL - 1) // UNROLL, step, 0)
    for c in range(columns):
        out[:, c * size : (c + 1) * size] = acc[c].astype(out.dtype)


def shards(sizes, n_cols, activations, blocks_one, pattern_one, count_one, blocks_two, pattern_two, count_two):
    depth, width, cores = sizes
    n_rows = depth * width * cores
    own_rows, features = activations.shape
    slots, size = blocks_one.shape[2], blocks_one.shape[3]
    columns_one = features * n_rows // n_cols // size
    columns_two = features // size
    groups = max(1, n_rows // columns_one)
    units = columns_one * groups
    per = units // (width * cores)
    each = per // depth
    smem = pl.BlockSpec(memory_space=pltpu.SMEM)
    vmem = pl.BlockSpec(memory_space=pltpu.VMEM)
    anyspace = pl.BlockSpec(memory_space=pl.ANY)

    def move(value, which, by):
        return lax.ppermute(value, "row", digit_shift(sizes, which, by))

    def across(value, by):
        return lax.ppermute(value, "col", [(b, (b + by) % n_cols) for b in range(n_cols)])

    def call(kernel, outs, scalars, arrays, scratch=(), rows=0, load=0):
        total = sum(a.size * a.dtype.itemsize for a in (*arrays, *outs, *scratch))
        cost = None
        if rows:
            cost = pl.CostEstimate(
                flops=2 * slots * rows * size * size, bytes_accessed=slots * size * size * 2, transcendentals=0
            )
        return pl.pallas_call(
            kernel,
            out_shape=tuple(outs),
            in_specs=[smem] * len(scalars) + [anyspace if load else vmem] * len(arrays),
            out_specs=(vmem,) * len(outs),
            scratch_shapes=[pltpu.VMEM(a.shape, a.dtype) for a in scratch] + [pltpu.SemaphoreType.DMA((load,))] * bool(load),
            compiler_params=pltpu.CompilerParams(vmem_limit_bytes=total + SPARE),
            cost_estimate=cost,
        )(*scalars, *arrays)

    def first(act, stored):
        load = stored is None
        rows = act.shape[0]
        m = rows // groups
        half = (units // cores, m, size)
        outs = [jax.ShapeDtypeStruct(half, SEND), jax.ShapeDtypeStruct(half, jnp.float32)]
        if load:
            act = pltpu.with_memory_space_constraint(act, pltpu.HBM)
            stored = pltpu.with_memory_space_constraint(blocks_one.reshape(slots, size, size), pltpu.HBM)
            outs.append(jax.ShapeDtypeStruct(stored.shape, stored.dtype))
        return call(
            functools.partial(first_kernel, sizes, groups, load),
            outs,
            [pattern_one.reshape(1, slots), count_one],
            [act, stored],
            [
                jax.ShapeDtypeStruct((columns_two, rows, size), jnp.bfloat16),
                jax.ShapeDtypeStruct((units + groups, m, size), jnp.float32),
            ],
            rows,
            (columns_two + 1) * load,
        )

    def spread(arrays, which):
        n = sizes[which]
        arrays = [a.reshape((n, a.shape[0] // n) + a.shape[1:]) for a in arrays]
        shape = arrays[0].shape[1:]
        kinds = [jnp.float32] + [jnp.bfloat16] * (n - 1)
        outs = call(
            functools.partial(spread_kernel, sizes, which),
            [jax.ShapeDtypeStruct(shape, kind) for kind in kinds],
            [],
            arrays,
        )
        return [outs[0]] + [move(out, which, k + 1) for k, out in enumerate(outs[1:])]

    def reduce_core(pair):
        send, keep = pair
        return [keep, move(send, 2, 1)]

    def reduce_width(arrays):
        return spread(arrays, 1)

    def reduce_depth(arrays):
        arrays = spread(arrays, 0)
        return call(finish_kernel, [jax.ShapeDtypeStruct(arrays[0].shape, jnp.bfloat16)], [], arrays)[0]

    def gather_depth(hidden):
        arrays = [hidden] + [move(hidden, 0, k) for k in range(1, depth)]
        joined = (depth * each,) + hidden.shape[1:]
        return call(join_kernel, [jax.ShapeDtypeStruct(joined, jnp.bfloat16)], [], arrays)[0]

    def gather_width(line):
        far = [move(line, 1, k) for k in range(1, width)]
        near = [move(line, 2, k) for k in range(1, cores)]
        return [line, *far] + [p for k in range(1, cores) for p in (near[k - 1], *(move(f, 2, k) for f in far))]

    def second(pieces, out_type):
        rows = pieces[0].shape[1] * groups
        return call(
            functools.partial(second_kernel, sizes, groups),
            [jax.ShapeDtypeStruct((rows, features), out_type)],
            [pattern_two.reshape(1, slots), count_two],
            [*pieces, blocks_two.reshape(slots, size, size)],
            [jax.ShapeDtypeStruct((columns_two + 1, rows, size), jnp.float32)],
            rows if out_type == jnp.bfloat16 else 0,
        )[0]

    theirs = [across(activations, k) for k in range(1, n_cols)]
    theirs = theirs[0] if n_cols == 2 else jnp.concatenate(theirs, axis=0)
    send, keep, stored = first(activations, None)
    own = (send, keep)
    theirs = first(theirs, stored)
    chunks = {"theirs": theirs, "own": own}
    stages = {
        "reduce_core": reduce_core,
        "reduce_width": reduce_width,
        "reduce_depth": reduce_depth,
        "gather_depth": gather_depth,
        "gather_width": gather_width,
    }
    for run in stages.values():
        for name in chunks:
            chunks[name] = run(chunks[name])
    rest = second(chunks["theirs"], jnp.bfloat16)
    mine = second(chunks["own"], jnp.float32)
    for k in range(1, n_cols):
        back = across(lax.slice_in_dim(rest, (k - 1) * own_rows, k * own_rows, axis=0), -k)
        mine = mine + back.astype(jnp.float32)
    return jnp.maximum(mine + bias_value, 0.0).astype(jnp.bfloat16)


def solution(mesh):
    n_rows, n_cols = mesh.shape["row"], mesh.shape["col"]
    sizes = (DEPTH, n_rows // (DEPTH * CORES), CORES)
    in_specs = (
        P("col", "row"),
        P("row", "col", None, None, None),
        P("row", "col", None),
        P("row", "col"),
        P("col", "row", None, None, None),
        P("col", "row", None),
        P("col", "row"),
    )
    return jax.shard_map(
        functools.partial(shards, sizes, n_cols),
        mesh=mesh,
        in_specs=in_specs,
        out_specs=P("col", "row"),
        check_vma=False,
    )
```

profile of v0, /device:TPU:0, one launch (start us, length us, event | category | flops | bytes accessed | tf_op | source)
XLA Modules:
  0.0 75.0 jit_solution(16736267592067700878)
XLA Ops:
  0.0 3.0 %collective-permute-start.11 = (bf16[64,1024]{1,0:T(8,128)(2,1)}, bf16[64,1024]{1,0:T(8,128)(2,1)S(1)}, u32[]{:S(2)}, u32[]{:S(2)}) collective-permute-start(bf16[64,1024]{1,0:T(8,128)(2,1)} %act.1), channel_id=1, source_target_pairs={{0,1},{1,0},{2,3},{3,2},{4,5},{5,4},{6,7},{7,6},{8,9},{9,8},{10,11... | collective-permute-start | bytes 393224 | tf_op jit(solution)/shard_map/ppermute | solution.py:214
  3.7 0.6 copy-done.2
  4.3 2.7 %shard_map.73 = (f32[32,64,128]{2,1,0:T(8,128)S(1)}, f32[32,64,128]{2,1,0:T(8,128)S(1)}, bf16[64,128,128]{2,1,0:T(8,128)(2,1)S(1)}) custom-call(s32[1,64]{1,0:T(1,128)S(1)} %bitcast.24, s32[1,1]{1,0:T(1,128)S(6)} %copy.8.count, bf16[64,1024]{1,0:T(8,128)(2,1)} %act.1, bf16[64,128,128]{2,1,0:T(8,128)(2,1)} %bitcast.26), custom_call_target="tpu_custom_call" | custom-call | flops 134217728 | bytes 2097152 | tf_op jit(solution)/shard_map/pallas_call | solution.py:223
  7.0 1.1 %shard_map.79 = (f32[32,64,128]{2,1,0:T(8,128)S(1)}, f32[32,64,128]{2,1,0:T(8,128)S(1)}) custom-call(s32[1,64]{1,0:T(1,128)S(1)} %bitcast.25, s32[1,1]{1,0:T(1,128)S(6)} %copy.8.count, bf16[64,1024]{1,0:T(8,128)(2,1)S(1)} %collective-permute-done.11.act, bf16[64,128,128]{2,1,0:T(8,128)(2,1)S(1)} %get-tuple-element.30.blocks), custom_call_target="tpu_custom_call" | custom-call | flops 134217728 | bytes 2097152 | tf_op jit(solution)/shard_map/pallas_call | solution.py:223
  8.7 2.1 %collective-permute-done.12 = f32[32,64,128]{2,1,0:T(8,128)S(1)} collective-permute-done((f32[32,64,128]{2,1,0:T(8,128)S(1)}, f32[32,64,128]{2,1,0:T(8,128)S(1)}, u32[]{:S(2)}, u32[]{:S(2)}) %collective-permute-start.12) | collective-permute-done | bytes 1048608 | tf_op jit(solution)/shard_map/ppermute | solution.py:211
  11.0 2.4 %collective-permute-start.13 = (bf16[16,64,128]{2,1,0:T(8,128)(2,1)S(1)}, bf16[16,64,128]{2,1,0:T(8,128)(2,1)S(1)}, u32[]{:S(2)}, u32[]{:S(2)}) collective-permute-start(bf16[16,64,128]{2,1,0:T(8,128)(2,1)S(1)} %get-tuple-element.34), channel_id=1, source_target_pairs={{0,4},{2,6},{4,0},{6,2},{8,12},{10,14},{12,8},{14,10},{16,20},{18,... | collective-permute-start | bytes 786440 | tf_op jit(solution)/shard_map/ppermute | solution.py:211
  13.6 1.3 %collective-permute-start.1 = (bf16[16,64,128]{2,1,0:T(8,128)(2,1)S(1)}, bf16[16,64,128]{2,1,0:T(8,128)(2,1)S(1)}, u32[]{:S(2)}, u32[]{:S(2)}) collective-permute-start(bf16[16,64,128]{2,1,0:T(8,128)(2,1)S(1)} %get-tuple-element.25), channel_id=1, source_target_pairs={{0,4},{2,6},{4,0},{6,2},{8,12},{10,14},{12,8},{14,10},{16,20},{18,... | collective-permute-start | bytes 786440 | tf_op jit(solution)/shard_map/ppermute | solution.py:211
  14.9 5.6 %collective-permute-done.13 = bf16[16,64,128]{2,1,0:T(8,128)(2,1)S(1)} collective-permute-done((bf16[16,64,128]{2,1,0:T(8,128)(2,1)S(1)}, bf16[16,64,128]{2,1,0:T(8,128)(2,1)S(1)}, u32[]{:S(2)}, u32[]{:S(2)}) %collective-permute-start.13) | collective-permute-done | bytes 262176 | tf_op jit(solution)/shard_map/ppermute | solution.py:211
  20.6 2.6 %collective-permute-start.14 = (bf16[4,64,128]{2,1,0:T(8,128)(2,1)S(1)}, bf16[4,64,128]{2,1,0:T(8,128)(2,1)S(1)}, u32[]{:S(2)}, u32[]{:S(2)}) collective-permute-start(bf16[4,64,128]{2,1,0:T(8,128)(2,1)S(1)} %get-tuple-element.36), channel_id=1, source_target_pairs={{0,8},{2,10},{4,12},{6,14},{8,0},{10,2},{12,4},{14,6},{16,24},{18,... | collective-permute-start | bytes 196616 | tf_op jit(solution)/shard_map/ppermute | solution.py:211
  23.2 2.5 %collective-permute-start.15 = (bf16[4,64,128]{2,1,0:T(8,128)(2,1)S(1)}, bf16[4,64,128]{2,1,0:T(8,128)(2,1)S(1)}, u32[]{:S(2)}, u32[]{:S(2)}) collective-permute-start(bf16[4,64,128]{2,1,0:T(8,128)(2,1)S(1)} %get-tuple-element.37), channel_id=1, source_target_pairs={{0,16},{2,18},{4,20},{6,22},{8,24},{10,26},{12,28},{14,30},{16,0},... | collective-permute-start | bytes 196616 | tf_op jit(solution)/shard_map/ppermute | solution.py:211
  26.1 2.3 %collective-permute-done.15.refs_2_ = bf16[4,64,128]{2,1,0:T(8,128)(2,1)S(1)} collective-permute-done((bf16[4,64,128]{2,1,0:T(8,128)(2,1)S(1)}, bf16[4,64,128]{2,1,0:T(8,128)(2,1)S(1)}, u32[]{:S(2)}, u32[]{:S(2)}) %collective-permute-start.15) | collective-permute-done | bytes 65568 | tf_op jit(solution)/shard_map/ppermute | solution.py:211
  28.4 3.6 %collective-permute-done.16.refs_3_ = bf16[4,64,128]{2,1,0:T(8,128)(2,1)S(1)} collective-permute-done((bf16[4,64,128]{2,1,0:T(8,128)(2,1)S(1)}, bf16[4,64,128]{2,1,0:T(8,128)(2,1)S(1)}, u32[]{:S(2)}, u32[]{:S(2)}) %collective-permute-start.16) | collective-permute-done | bytes 65568 | tf_op jit(solution)/shard_map/ppermute | solution.py:211
  32.2 1.3 %collective-permute-start.18 = (bf16[4,64,128]{2,1,0:T(8,128)(2,1)S(1)}, bf16[4,64,128]{2,1,0:T(8,128)(2,1)S(1)}, u32[]{:S(2)}, u32[]{:S(2)}) collective-permute-start(bf16[4,64,128]{2,1,0:T(8,128)(2,1)S(1)} %shard_map.82.refs_0_), channel_id=1, source_target_pairs={{0,16},{2,18},{4,20},{6,22},{8,24},{10,26},{12,28},{14,30},{16,0},... | collective-permute-start | bytes 196616 | tf_op jit(solution)/shard_map/ppermute | solution.py:211
  33.5 3.1 %collective-permute-start.19 = (bf16[4,64,128]{2,1,0:T(8,128)(2,1)S(1)}, bf16[4,64,128]{2,1,0:T(8,128)(2,1)S(1)}, u32[]{:S(2)}, u32[]{:S(2)}) collective-permute-start(bf16[4,64,128]{2,1,0:T(8,128)(2,1)S(1)} %shard_map.82.refs_0_), channel_id=1, source_target_pairs={{0,24},{2,26},{4,28},{6,30},{8,16},{10,18},{12,20},{14,22},{16,8},... | collective-permute-start | bytes 196616 | tf_op jit(solution)/shard_map/ppermute | solution.py:211
  36.6 0.8 %collective-permute-done.18.refs_2_ = bf16[4,64,128]{2,1,0:T(8,128)(2,1)S(1)} collective-permute-done((bf16[4,64,128]{2,1,0:T(8,128)(2,1)S(1)}, bf16[4,64,128]{2,1,0:T(8,128)(2,1)S(1)}, u32[]{:S(2)}, u32[]{:S(2)}) %collective-permute-start.18) | collective-permute-done | bytes 65568 | tf_op jit(solution)/shard_map/ppermute | solution.py:211
  37.4 2.2 %collective-permute-done.19.refs_3_ = bf16[4,64,128]{2,1,0:T(8,128)(2,1)S(1)} collective-permute-done((bf16[4,64,128]{2,1,0:T(8,128)(2,1)S(1)}, bf16[4,64,128]{2,1,0:T(8,128)(2,1)S(1)}, u32[]{:S(2)}, u32[]{:S(2)}) %collective-permute-start.19) | collective-permute-done | bytes 65568 | tf_op jit(solution)/shard_map/ppermute | solution.py:211
  39.6 2.3 %collective-permute-start.20 = (bf16[16,64,128]{2,1,0:T(8,128)(2,1)S(1)}, bf16[16,64,128]{2,1,0:T(8,128)(2,1)S(1)}, u32[]{:S(2)}, u32[]{:S(2)}) collective-permute-start(bf16[16,64,128]{2,1,0:T(8,128)(2,1)S(1)} %shard_map.83.refs_0_), channel_id=1, source_target_pairs={{0,4},{2,6},{4,0},{6,2},{8,12},{10,14},{12,8},{14,10},{16,20},{18,... | collective-permute-start | bytes 786440 | tf_op jit(solution)/shard_map/ppermute | solution.py:211
  42.1 3.7 %collective-permute-start.3 = (bf16[4,64,128]{2,1,0:T(8,128)(2,1)S(1)}, bf16[4,64,128]{2,1,0:T(8,128)(2,1)S(1)}, u32[]{:S(2)}, u32[]{:S(2)}) collective-permute-start(bf16[4,64,128]{2,1,0:T(8,128)(2,1)S(1)} %get-tuple-element.28), channel_id=1, source_target_pairs={{0,16},{2,18},{4,20},{6,22},{8,24},{10,26},{12,28},{14,30},{16,0},... | collective-permute-start | bytes 196616 | tf_op jit(solution)/shard_map/ppermute | solution.py:211
  45.7 0.7 collective-permute-start.4
  46.5 1.6 %collective-permute-done.3.refs_2_ = bf16[4,64,128]{2,1,0:T(8,128)(2,1)S(1)} collective-permute-done((bf16[4,64,128]{2,1,0:T(8,128)(2,1)S(1)}, bf16[4,64,128]{2,1,0:T(8,128)(2,1)S(1)}, u32[]{:S(2)}, u32[]{:S(2)}) %collective-permute-start.3) | collective-permute-done | bytes 65568 | tf_op jit(solution)/shard_map/ppermute | solution.py:211
  48.1 3.7 %collective-permute-done.4.refs_3_ = bf16[4,64,128]{2,1,0:T(8,128)(2,1)S(1)} collective-permute-done((bf16[4,64,128]{2,1,0:T(8,128)(2,1)S(1)}, bf16[4,64,128]{2,1,0:T(8,128)(2,1)S(1)}, u32[]{:S(2)}, u32[]{:S(2)}) %collective-permute-start.4) | collective-permute-done | bytes 65568 | tf_op jit(solution)/shard_map/ppermute | solution.py:211
  51.8 1.3 %collective-permute-start.5 = (bf16[4,64,128]{2,1,0:T(8,128)(2,1)S(1)}, bf16[4,64,128]{2,1,0:T(8,128)(2,1)S(1)}, u32[]{:S(2)}, u32[]{:S(2)}) collective-permute-start(bf16[4,64,128]{2,1,0:T(8,128)(2,1)S(1)} %shard_map.76.refs_0_), channel_id=1, source_target_pairs={{0,8},{2,10},{4,12},{6,14},{8,0},{10,2},{12,4},{14,6},{16,24},{18,... | collective-permute-start | bytes 196616 | tf_op jit(solution)/shard_map/ppermute | solution.py:211
  53.1 1.2 %collective-permute-start.6 = (bf16[4,64,128]{2,1,0:T(8,128)(2,1)S(1)}, bf16[4,64,128]{2,1,0:T(8,128)(2,1)S(1)}, u32[]{:S(2)}, u32[]{:S(2)}) collective-permute-start(bf16[4,64,128]{2,1,0:T(8,128)(2,1)S(1)} %shard_map.76.refs_0_), channel_id=1, source_target_pairs={{0,16},{2,18},{4,20},{6,22},{8,24},{10,26},{12,28},{14,30},{16,0},... | collective-permute-start | bytes 196616 | tf_op jit(solution)/shard_map/ppermute | solution.py:211
  54.3 2.0 %collective-permute-start.7 = (bf16[4,64,128]{2,1,0:T(8,128)(2,1)S(1)}, bf16[4,64,128]{2,1,0:T(8,128)(2,1)S(1)}, u32[]{:S(2)}, u32[]{:S(2)}) collective-permute-start(bf16[4,64,128]{2,1,0:T(8,128)(2,1)S(1)} %shard_map.76.refs_0_), channel_id=1, source_target_pairs={{0,24},{2,26},{4,28},{6,30},{8,16},{10,18},{12,20},{14,22},{16,8},... | collective-permute-start | bytes 196616 | tf_op jit(solution)/shard_map/ppermute | solution.py:211
  56.3 2.7 %collective-permute-done.6.refs_2_ = bf16[4,64,128]{2,1,0:T(8,128)(2,1)S(1)} collective-permute-done((bf16[4,64,128]{2,1,0:T(8,128)(2,1)S(1)}, bf16[4,64,128]{2,1,0:T(8,128)(2,1)S(1)}, u32[]{:S(2)}, u32[]{:S(2)}) %collective-permute-start.6) | collective-permute-done | bytes 65568 | tf_op jit(solution)/shard_map/ppermute | solution.py:211
  59.0 1.5 %collective-permute-done.7.refs_3_ = bf16[4,64,128]{2,1,0:T(8,128)(2,1)S(1)} collective-permute-done((bf16[4,64,128]{2,1,0:T(8,128)(2,1)S(1)}, bf16[4,64,128]{2,1,0:T(8,128)(2,1)S(1)}, u32[]{:S(2)}, u32[]{:S(2)}) %collective-permute-start.7) | collective-permute-done | bytes 65568 | tf_op jit(solution)/shard_map/ppermute | solution.py:211
  61.3 5.7 %collective-permute-done.8.refs_1_ = bf16[16,64,128]{2,1,0:T(8,128)(2,1)S(1)} collective-permute-done((bf16[16,64,128]{2,1,0:T(8,128)(2,1)S(1)}, bf16[16,64,128]{2,1,0:T(8,128)(2,1)S(1)}, u32[]{:S(2)}, u32[]{:S(2)}) %collective-permute-start.8) | collective-permute-done | bytes 262176 | tf_op jit(solution)/shard_map/ppermute | solution.py:211
  67.6 1.0 %shard_map.84 = bf16[64,1024]{1,0:T(8,128)(2,1)S(1)} custom-call(s32[1,64]{1,0:T(1,128)S(1)} %bitcast.22, s32[1,1]{1,0:T(1,128)S(6)} %copy.9.count, bf16[16,64,128]{2,1,0:T(8,128)(2,1)S(1)} %shard_map.83.refs_0_, bf16[16,64,128]{2,1,0:T(8,128)(2,1)S(1)} %collective-permute-done.20.refs_1_, bf16[16,64,128]{2,1,0:T(8,128)(2,1)S(1)} %collective-permute-done.21.refs_2_, ...), custom_call_target="tpu_custom_call" | custom-call | flops 134217728 | bytes 2097152 | tf_op jit(solution)/shard_map/pallas_call | solution.py:223
  68.7 0.6 collective-permute-start.23
  69.3 1.0 %shard_map.78 = f32[64,1024]{1,0:T(8,128)S(1)} custom-call(s32[1,64]{1,0:T(1,128)S(1)} %bitcast.23, s32[1,1]{1,0:T(1,128)S(6)} %copy.9.count, bf16[16,64,128]{2,1,0:T(8,128)(2,1)S(1)} %shard_map.77.refs_0_, bf16[16,64,128]{2,1,0:T(8,128)(2,1)S(1)} %collective-permute-done.8.refs_1_, bf16[16,64,128]{2,1,0:T(8,128)(2,1)S(1)} %collective-permute-done.9.refs_2_, ...), custom_call_target="tpu_custom_call" | custom-call | tf_op jit(solution)/shard_map/pallas_call | solution.py:223
  70.3 3.9 %collective-permute-done.23 = bf16[64,1024]{1,0:T(8,128)(2,1)S(1)} collective-permute-done((bf16[64,1024]{1,0:T(8,128)(2,1)S(1)}, bf16[64,1024]{1,0:T(8,128)(2,1)S(1)}, u32[]{:S(2)}, u32[]{:S(2)}) %collective-permute-start.23) | collective-permute-done | bytes 131104 | tf_op jit(solution)/shard_map/ppermute | solution.py:214
  74.3 0.7 maximum_convert_fusion
  (35 shorter events, 2.5 us)
Async XLA Ops:
  0.0 7.0 %collective-permute-start.11 = (bf16[64,1024]{1,0:T(8,128)(2,1)}, bf16[64,1024]{1,0:T(8,128)(2,1)S(1)}, u32[]{:S(2)}, u32[]{:S(2)}) collective-permute-start(bf16[64,1024]{1,0:T(8,128)(2,1)} %act.1), channel_id=1, source_target_pairs={{0,1},{1,0},{2,3},{3,2},{4,5},{5,4},{6,7},{7,6},{8,9},{9,8},{10,11... | collective-permute-start | bytes 393224 | tf_op jit(solution)/shard_map/ppermute | solution.py:214
  3.6 0.7 copy-start.2
  8.1 2.7 %collective-permute-start.12 = (f32[32,64,128]{2,1,0:T(8,128)S(1)}, f32[32,64,128]{2,1,0:T(8,128)S(1)}, u32[]{:S(2)}, u32[]{:S(2)}) collective-permute-start(f32[32,64,128]{2,1,0:T(8,128)S(1)} %get-tuple-element.32), channel_id=1, source_target_pairs={{0,2},{2,0},{4,6},{6,4},{8,10},{10,8},{12,14},{14,12},{16,18},{18,... | collective-permute-start | bytes 3145736 | tf_op jit(solution)/shard_map/ppermute | solution.py:211
  8.2 5.2 %collective-permute-start = (f32[32,64,128]{2,1,0:T(8,128)S(1)}, f32[32,64,128]{2,1,0:T(8,128)S(1)}, u32[]{:S(2)}, u32[]{:S(2)}) collective-permute-start(f32[32,64,128]{2,1,0:T(8,128)S(1)} %get-tuple-element.23), channel_id=1, source_target_pairs={{0,2},{2,0},{4,6},{6,4},{8,10},{10,8},{12,14},{14,12},{16,18},{18,... | collective-permute-start | bytes 3145736 | tf_op jit(solution)/shard_map/ppermute | solution.py:211
  11.0 9.5 %collective-permute-start.13 = (bf16[16,64,128]{2,1,0:T(8,128)(2,1)S(1)}, bf16[16,64,128]{2,1,0:T(8,128)(2,1)S(1)}, u32[]{:S(2)}, u32[]{:S(2)}) collective-permute-start(bf16[16,64,128]{2,1,0:T(8,128)(2,1)S(1)} %get-tuple-element.34), channel_id=1, source_target_pairs={{0,4},{2,6},{4,0},{6,2},{8,12},{10,14},{12,8},{14,10},{16,20},{18,... | collective-permute-start | bytes 786440 | tf_op jit(solution)/shard_map/ppermute | solution.py:211
  13.6 54.1 %copy-start = (bf16[1,1,64,128,128]{4,3,2,1,0:T(8,128)(2,1)S(1)}, bf16[1,1,64,128,128]{4,3,2,1,0:T(8,128)(2,1)}, u32[]{:S(2)}) copy-start(bf16[1,1,64,128,128]{4,3,2,1,0:T(8,128)(2,1)} %param.11) | copy-start | bytes 6291460
  13.6 54.1 %copy-start.1 = (s32[1,1,64]{2,1,0:T(1,128)S(1)}, s32[1,1,64]{2,1,0:T(1,128)}, u32[]{:S(2)}) copy-start(s32[1,1,64]{2,1,0:T(1,128)} %param.12) | copy-start | bytes 772
  13.6 28.3 %collective-permute-start.1 = (bf16[16,64,128]{2,1,0:T(8,128)(2,1)S(1)}, bf16[16,64,128]{2,1,0:T(8,128)(2,1)S(1)}, u32[]{:S(2)}, u32[]{:S(2)}) collective-permute-start(bf16[16,64,128]{2,1,0:T(8,128)(2,1)S(1)} %get-tuple-element.25), channel_id=1, source_target_pairs={{0,4},{2,6},{4,0},{6,2},{8,12},{10,14},{12,8},{14,10},{16,20},{18,... | collective-permute-start | bytes 786440 | tf_op jit(solution)/shard_map/ppermute | solution.py:211
  20.6 5.5 %collective-permute-start.14 = (bf16[4,64,128]{2,1,0:T(8,128)(2,1)S(1)}, bf16[4,64,128]{2,1,0:T(8,128)(2,1)S(1)}, u32[]{:S(2)}, u32[]{:S(2)}) collective-permute-start(bf16[4,64,128]{2,1,0:T(8,128)(2,1)S(1)} %get-tuple-element.36), channel_id=1, source_target_pairs={{0,8},{2,10},{4,12},{6,14},{8,0},{10,2},{12,4},{14,6},{16,24},{18,... | collective-permute-start | bytes 196616 | tf_op jit(solution)/shard_map/ppermute | solution.py:211
  23.2 5.2 %collective-permute-start.15 = (bf16[4,64,128]{2,1,0:T(8,128)(2,1)S(1)}, bf16[4,64,128]{2,1,0:T(8,128)(2,1)S(1)}, u32[]{:S(2)}, u32[]{:S(2)}) collective-permute-start(bf16[4,64,128]{2,1,0:T(8,128)(2,1)S(1)} %get-tuple-element.37), channel_id=1, source_target_pairs={{0,16},{2,18},{4,20},{6,22},{8,24},{10,26},{12,28},{14,30},{16,0},... | collective-permute-start | bytes 196616 | tf_op jit(solution)/shard_map/ppermute | solution.py:211
  25.7 6.3 %collective-permute-start.16 = (bf16[4,64,128]{2,1,0:T(8,128)(2,1)S(1)}, bf16[4,64,128]{2,1,0:T(8,128)(2,1)S(1)}, u32[]{:S(2)}, u32[]{:S(2)}) collective-permute-start(bf16[4,64,128]{2,1,0:T(8,128)(2,1)S(1)} %get-tuple-element.38), channel_id=1, source_target_pairs={{0,24},{2,26},{4,28},{6,30},{8,16},{10,18},{12,20},{14,22},{16,8},... | collective-permute-start | bytes 196616 | tf_op jit(solution)/shard_map/ppermute | solution.py:211
  32.1 4.5 %collective-permute-start.17 = (bf16[4,64,128]{2,1,0:T(8,128)(2,1)S(1)}, bf16[4,64,128]{2,1,0:T(8,128)(2,1)S(1)}, u32[]{:S(2)}, u32[]{:S(2)}) collective-permute-start(bf16[4,64,128]{2,1,0:T(8,128)(2,1)S(1)} %shard_map.82.refs_0_), channel_id=1, source_target_pairs={{0,8},{2,10},{4,12},{6,14},{8,0},{10,2},{12,4},{14,6},{16,24},{18,... | collective-permute-start | bytes 196616 | tf_op jit(solution)/shard_map/ppermute | solution.py:211
  32.2 5.2 %collective-permute-start.18 = (bf16[4,64,128]{2,1,0:T(8,128)(2,1)S(1)}, bf16[4,64,128]{2,1,0:T(8,128)(2,1)S(1)}, u32[]{:S(2)}, u32[]{:S(2)}) collective-permute-start(bf16[4,64,128]{2,1,0:T(8,128)(2,1)S(1)} %shard_map.82.refs_0_), channel_id=1, source_target_pairs={{0,16},{2,18},{4,20},{6,22},{8,24},{10,26},{12,28},{14,30},{16,0},... | collective-permute-start | bytes 196616 | tf_op jit(solution)/shard_map/ppermute | solution.py:211
  33.5 6.1 %collective-permute-start.19 = (bf16[4,64,128]{2,1,0:T(8,128)(2,1)S(1)}, bf16[4,64,128]{2,1,0:T(8,128)(2,1)S(1)}, u32[]{:S(2)}, u32[]{:S(2)}) collective-permute-start(bf16[4,64,128]{2,1,0:T(8,128)(2,1)S(1)} %shard_map.82.refs_0_), channel_id=1, source_target_pairs={{0,24},{2,26},{4,28},{6,30},{8,16},{10,18},{12,20},{14,22},{16,8},... | collective-permute-start | bytes 196616 | tf_op jit(solution)/shard_map/ppermute | solution.py:211
  39.6 21.0 %collective-permute-start.20 = (bf16[16,64,128]{2,1,0:T(8,128)(2,1)S(1)}, bf16[16,64,128]{2,1,0:T(8,128)(2,1)S(1)}, u32[]{:S(2)}, u32[]{:S(2)}) collective-permute-start(bf16[16,64,128]{2,1,0:T(8,128)(2,1)S(1)} %shard_map.83.refs_0_), channel_id=1, source_target_pairs={{0,4},{2,6},{4,0},{6,2},{8,12},{10,14},{12,8},{14,10},{16,20},{18,... | collective-permute-start | bytes 786440 | tf_op jit(solution)/shard_map/ppermute | solution.py:211
  42.0 4.5 %collective-permute-start.2 = (bf16[4,64,128]{2,1,0:T(8,128)(2,1)S(1)}, bf16[4,64,128]{2,1,0:T(8,128)(2,1)S(1)}, u32[]{:S(2)}, u32[]{:S(2)}) collective-permute-start(bf16[4,64,128]{2,1,0:T(8,128)(2,1)S(1)} %get-tuple-element.27), channel_id=1, source_target_pairs={{0,8},{2,10},{4,12},{6,14},{8,0},{10,2},{12,4},{14,6},{16,24},{18,... | collective-permute-start | bytes 196616 | tf_op jit(solution)/shard_map/ppermute | solution.py:211
  42.1 6.0 %collective-permute-start.3 = (bf16[4,64,128]{2,1,0:T(8,128)(2,1)S(1)}, bf16[4,64,128]{2,1,0:T(8,128)(2,1)S(1)}, u32[]{:S(2)}, u32[]{:S(2)}) collective-permute-start(bf16[4,64,128]{2,1,0:T(8,128)(2,1)S(1)} %get-tuple-element.28), channel_id=1, source_target_pairs={{0,16},{2,18},{4,20},{6,22},{8,24},{10,26},{12,28},{14,30},{16,0},... | collective-permute-start | bytes 196616 | tf_op jit(solution)/shard_map/ppermute | solution.py:211
  45.7 6.1 %collective-permute-start.4 = (bf16[4,64,128]{2,1,0:T(8,128)(2,1)S(1)}, bf16[4,64,128]{2,1,0:T(8,128)(2,1)S(1)}, u32[]{:S(2)}, u32[]{:S(2)}) collective-permute-start(bf16[4,64,128]{2,1,0:T(8,128)(2,1)S(1)} %get-tuple-element.29), channel_id=1, source_target_pairs={{0,24},{2,26},{4,28},{6,30},{8,16},{10,18},{12,20},{14,22},{16,8},... | collective-permute-start | bytes 196616 | tf_op jit(solution)/shard_map/ppermute | solution.py:211
  51.8 4.5 %collective-permute-start.5 = (bf16[4,64,128]{2,1,0:T(8,128)(2,1)S(1)}, bf16[4,64,128]{2,1,0:T(8,128)(2,1)S(1)}, u32[]{:S(2)}, u32[]{:S(2)}) collective-permute-start(bf16[4,64,128]{2,1,0:T(8,128)(2,1)S(1)} %shard_map.76.refs_0_), channel_id=1, source_target_pairs={{0,8},{2,10},{4,12},{6,14},{8,0},{10,2},{12,4},{14,6},{16,24},{18,... | collective-permute-start | bytes 196616 | tf_op jit(solution)/shard_map/ppermute | solution.py:211
  53.1 5.9 %collective-permute-start.6 = (bf16[4,64,128]{2,1,0:T(8,128)(2,1)S(1)}, bf16[4,64,128]{2,1,0:T(8,128)(2,1)S(1)}, u32[]{:S(2)}, u32[]{:S(2)}) collective-permute-start(bf16[4,64,128]{2,1,0:T(8,128)(2,1)S(1)} %shard_map.76.refs_0_), channel_id=1, source_target_pairs={{0,16},{2,18},{4,20},{6,22},{8,24},{10,26},{12,28},{14,30},{16,0},... | collective-permute-start | bytes 196616 | tf_op jit(solution)/shard_map/ppermute | solution.py:211
  54.3 6.2 %collective-permute-start.7 = (bf16[4,64,128]{2,1,0:T(8,128)(2,1)S(1)}, bf16[4,64,128]{2,1,0:T(8,128)(2,1)S(1)}, u32[]{:S(2)}, u32[]{:S(2)}) collective-permute-start(bf16[4,64,128]{2,1,0:T(8,128)(2,1)S(1)} %shard_map.76.refs_0_), channel_id=1, source_target_pairs={{0,24},{2,26},{4,28},{6,30},{8,16},{10,18},{12,20},{14,22},{16,8},... | collective-permute-start | bytes 196616 | tf_op jit(solution)/shard_map/ppermute | solution.py:211
  60.5 6.4 %collective-permute-start.8 = (bf16[16,64,128]{2,1,0:T(8,128)(2,1)S(1)}, bf16[16,64,128]{2,1,0:T(8,128)(2,1)S(1)}, u32[]{:S(2)}, u32[]{:S(2)}) collective-permute-start(bf16[16,64,128]{2,1,0:T(8,128)(2,1)S(1)} %shard_map.77.refs_0_), channel_id=1, source_target_pairs={{0,4},{2,6},{4,0},{6,2},{8,12},{10,14},{12,8},{14,10},{16,20},{18,... | collective-permute-start | bytes 786440 | tf_op jit(solution)/shard_map/ppermute | solution.py:211
  60.6 7.0 %collective-permute-start.21 = (bf16[16,64,128]{2,1,0:T(8,128)(2,1)S(1)}, bf16[16,64,128]{2,1,0:T(8,128)(2,1)S(1)}, u32[]{:S(2)}, u32[]{:S(2)}) collective-permute-start(bf16[16,64,128]{2,1,0:T(8,128)(2,1)S(1)} %shard_map.83.refs_0_), channel_id=1, source_target_pairs={{0,2},{2,0},{4,6},{6,4},{8,10},{10,8},{12,14},{14,12},{16,18},{18,... | collective-permute-start | bytes 786440 | tf_op jit(solution)/shard_map/ppermute | solution.py:211
  60.7 6.9 %collective-permute-start.22 = (bf16[16,64,128]{2,1,0:T(8,128)(2,1)S(1)}, bf16[16,64,128]{2,1,0:T(8,128)(2,1)S(1)}, u32[]{:S(2)}, u32[]{:S(2)}) collective-permute-start(bf16[16,64,128]{2,1,0:T(8,128)(2,1)S(1)} %collective-permute-done.20.refs_1_), channel_id=1, source_target_pairs={{0,2},{2,0},{4,6},{6,4},{8,10},{10,8},{12,14},{14,12},{16,18},{18,... | collective-permute-start | bytes 786440 | tf_op jit(solution)/shard_map/ppermute | solution.py:211
  61.2 8.1 %collective-permute-start.9 = (bf16[16,64,128]{2,1,0:T(8,128)(2,1)S(1)}, bf16[16,64,128]{2,1,0:T(8,128)(2,1)S(1)}, u32[]{:S(2)}, u32[]{:S(2)}) collective-permute-start(bf16[16,64,128]{2,1,0:T(8,128)(2,1)S(1)} %shard_map.77.refs_0_), channel_id=1, source_target_pairs={{0,2},{2,0},{4,6},{6,4},{8,10},{10,8},{12,14},{14,12},{16,18},{18,... | collective-permute-start | bytes 786440 | tf_op jit(solution)/shard_map/ppermute | solution.py:211
  66.9 2.4 %collective-permute-start.10 = (bf16[16,64,128]{2,1,0:T(8,128)(2,1)S(1)}, bf16[16,64,128]{2,1,0:T(8,128)(2,1)S(1)}, u32[]{:S(2)}, u32[]{:S(2)}) collective-permute-start(bf16[16,64,128]{2,1,0:T(8,128)(2,1)S(1)} %collective-permute-done.8.refs_1_), channel_id=1, source_target_pairs={{0,2},{2,0},{4,6},{6,4},{8,10},{10,8},{12,14},{14,12},{16,18},{18,... | collective-permute-start | bytes 786440 | tf_op jit(solution)/shard_map/ppermute | solution.py:211
  68.7 5.6 %collective-permute-start.23 = (bf16[64,1024]{1,0:T(8,128)(2,1)S(1)}, bf16[64,1024]{1,0:T(8,128)(2,1)S(1)}, u32[]{:S(2)}, u32[]{:S(2)}) collective-permute-start(bf16[64,1024]{1,0:T(8,128)(2,1)S(1)} %shard_map.84), channel_id=1, source_target_pairs={{0,1},{1,0},{2,3},{3,2},{4,5},{5,4},{6,7},{7,6},{8,9},{9,8},{10,11... | collective-permute-start | bytes 393224 | tf_op jit(solution)/shard_map/ppermute | solution.py:214
where the time goes:
time: 75.3 us; the launch traced here: 75 us
  waiting for transfers between devices  35.9 us (48%)
  starting transfers between devices  29.8 us (40%)
  Pallas kernels  6.38 us (8%)
  between operations  1.5 us (2%)
    ppermute x22, waiting for transfers between devices, move(): return lax.ppermute(value, 'row', digit_shift(sizes, which, by))  32 us
    ppermute x22, starting transfers between devices, move(): return lax.ppermute(value, 'row', digit_shift(sizes, which, by))  26.2 us
    pallas_call x12, Pallas kernels, call(): pl.pallas_call(kernel, out_shape=tuple(outs), in_specs=[smem] * len(scala...  6.38 us
    ppermute x2, waiting for transfers between devices, across(): lax.ppermute(value, 'col', [(b, (b + by) % n_cols) for b in range(n_cols)])  3.93 us
    ppermute x2, starting transfers between devices, across(): lax.ppermute(value, 'col', [(b, (b + by) % n_cols) for b in range(n_cols)])  3.62 us
  transfers between devices with their start and end apart: 24, of which 13 were waited for; matrix products, arithmetic and copies ran while one was open for 0% of the time, Pallas kernels for 7%

commit v1 on v0

--- a/solution.py
+++ b/solution.py
@@ -11,7 +11,7 @@
 bias_value = -0.3
 CORES = 2
 DEPTH = 4
-UNROLL = 8
+UNROLL = 16
 SEND = jnp.float32
 SPARE = 1024 * 1024
 
@@ -28,10 +28,10 @@
     return (digit + by) % size
 
 
-def behind(here, there, size):
+def sender(digit, by, size):
     if size & (size - 1) == 0:
-        return here ^ there
-    return (here - there + size) % size
+        return digit ^ by
+    return (digit + size - by) % size
 
 
 def digit_shift(sizes, which, by):
@@ -48,10 +48,10 @@
 
 
 def first_kernel(sizes, groups, load, pattern, count, act, blocks, *refs):
-    _, _, cores = sizes
+    _, width, cores = sizes
     _, size, _ = blocks.shape
     if load:
-        send, keep, held, stage, acc, sems = refs
+        held, stage, acc, sems = refs[2 * width :]
         copies = [
             pltpu.make_async_copy(act.at[:, pl.ds(r * size, size)], stage.at[r], sems.at[r])
             for r in range(stage.shape[0])
@@ -61,7 +61,7 @@
             copy.start()
         blocks = held
     else:
-        send, keep, stage, acc = refs
+        stage, acc = refs[2 * width :]
     units, m, _ = acc.shape
     units -= groups
     columns = units // groups
@@ -94,25 +94,33 @@
         return 0
 
     lax.fori_loop(0, (live + UNROLL - 1) // UNROLL, step, 0)
-    core = lax.axis_index("row") % cores
-    half = units // cores
-    mine = core * half
-    other = (cores - 1 - core) * half
-
-    def leave(u, _):
-        send[u] = acc[other + u].astype(send.dtype)
-        keep[u] = acc[mine + u]
-        return 0
-
-    lax.fori_loop(0, half, leave, 0, unroll=4)
-
-
-def spread_kernel(sizes, which, *refs):
-    size = sizes[which]
+    row = lax.axis_index("row")
+    core, x = row % cores, row // cores % width
+    per = units // (cores * width)
+    for k in range(width):
+        xd = turned(x, k, width)
+        mine = (core * width + xd) * per
+        other = ((cores - 1 - core) * width + xd) * per
+        send, keep = refs[k], refs[width + k]
+
+        def leave(u, _):
+            send[u] = acc[other + u].astype(send.dtype)
+            keep[u] = acc[mine + u]
+            return 0
+
+        lax.fori_loop(0, per, leave, 0, unroll=4)
+
+
+def pair_kernel(left, right, out):
+    def step(j, _):
+        out[j] = (left[j] + right[j].astype(jnp.float32)).astype(out.dtype)
+        return 0
+
+    lax.fori_loop(0, out.shape[0], step, 0, unroll=4)
+
+
+def spread_kernel(size, stride, *refs):
     arrays, outs = refs[:-size], refs[-size:]
-    stride = 1
-    for s in sizes[which + 1 :]:
-        stride *= s
     here = lax.axis_index("row") // stride % size
 
     def step(j, _):
@@ -148,28 +156,23 @@
 def second_kernel(sizes, groups, pattern, count, *refs):
     depth, width, cores = sizes
     pieces = refs[: width * cores]
-    blocks, out, acc = refs[width * cores :]
+    blocks, out, hidden, acc = refs[width * cores :]
     _, size, _ = blocks.shape
-    per, m, _ = pieces[0].shape
+    units, m, _ = hidden.shape
     columns = acc.shape[0] - 1
-    rows_in = per * width * cores // groups
-    each = per // depth
+    rows_in = units // groups
+    each = units // (depth * width * cores)
     live = count[0, 0]
     row = lax.axis_index("row")
     core, x, z = row % cores, row // cores % width, row // (cores * width)
     for c in range(columns):
         acc[c] = jnp.zeros(acc.shape[1:], jnp.float32)
-
-    def hidden(u):
-        rest, j = split(u, each)
-        rest, zd = split(rest, depth)
-        cd, xd = split(rest, width)
-        piece = behind(core, cd, cores) * width + behind(x, xd, width)
-        at = behind(z, zd, depth) * each + j
-        found = pieces[0][at]
-        for i in range(1, len(pieces)):
-            found = jnp.where(piece == i, pieces[i][at], found)
-        return found
+    for i, piece in enumerate(pieces):
+        cd, xd = sender(core, i // width, cores), sender(x, i % width, width)
+        for k in range(depth):
+            base = ((cd * width + xd) * depth + sender(z, k, depth)) * each
+            for j in range(each):
+                hidden[base + j] = piece[k * each + j]
 
     def step(t, _):
         base = t * UNROLL
@@ -178,7 +181,7 @@
             block = blocks[base + j]
             r, c = split(pattern[0, base + j], columns)
             products = [
-                jnp.dot(hidden(g * rows_in + r), block, preferred_element_type=jnp.float32) for g in range(groups)
+                jnp.dot(hidden[g * rows_in + r], block, preferred_element_type=jnp.float32) for g in range(groups)
             ]
             found.append((c, products))
         for j, (c, products) in enumerate(found):
@@ -234,8 +237,8 @@
         load = stored is None
         rows = act.shape[0]
         m = rows // groups
-        half = (units // cores, m, size)
-        outs = [jax.ShapeDtypeStruct(half, SEND), jax.ShapeDtypeStruct(half, jnp.float32)]
+        shape = (per, m, size)
+        outs = [jax.ShapeDtypeStruct(shape, kind) for kind in (SEND, jnp.float32) for _ in range(width)]
         if load:
             act = pltpu.with_memory_space_constraint(act, pltpu.HBM)
             stored = pltpu.with_memory_space_constraint(blocks_one.reshape(slots, size, size), pltpu.HBM)
@@ -253,28 +256,26 @@
             (columns_two + 1) * load,
         )
 
-    def spread(arrays, which):
-        n = sizes[which]
-        arrays = [a.reshape((n, a.shape[0] // n) + a.shape[1:]) for a in arrays]
-        shape = arrays[0].shape[1:]
-        kinds = [jnp.float32] + [jnp.bfloat16] * (n - 1)
-        outs = call(
-            functools.partial(spread_kernel, sizes, which),
-            [jax.ShapeDtypeStruct(shape, kind) for kind in kinds],
-            [],
-            arrays,
-        )
-        return [outs[0]] + [move(out, which, k + 1) for k, out in enumerate(outs[1:])]
-
-    def reduce_core(pair):
-        send, keep = pair
-        return [keep, move(send, 2, 1)]
-
-    def reduce_width(arrays):
-        return spread(arrays, 1)
+    def reduce_core(arrays):
+        steps = [*range(1, width), 0]
+        got = {}
+        for k in steps:
+            got[k] = move(arrays[k], 2, 1)
+        return [(arrays[width + k], got[k]) for k in range(width)]
+
+    def reduce_width(pairs):
+        gets = []
+        for k in range(1, width):
+            out = jax.ShapeDtypeStruct(pairs[k][0].shape, jnp.bfloat16)
+            gets.append(move(call(pair_kernel, [out], [], pairs[k])[0], 1, k))
+        return [*pairs[0], *gets]
 
     def reduce_depth(arrays):
-        arrays = spread(arrays, 0)
+        arrays = [a.reshape((depth, each) + a.shape[1:]) for a in arrays]
+        kinds = [jnp.float32] + [jnp.bfloat16] * (depth - 1)
+        outs = [jax.ShapeDtypeStruct(arrays[0].shape[1:], kind) for kind in kinds]
+        outs = call(functools.partial(spread_kernel, depth, width * cores), outs, [], arrays)
+        arrays = [outs[0]] + [move(out, 0, k + 1) for k, out in enumerate(outs[1:])]
         return call(finish_kernel, [jax.ShapeDtypeStruct(arrays[0].shape, jnp.bfloat16)], [], arrays)[0]
 
     def gather_depth(hidden):
@@ -294,14 +295,16 @@
             [jax.ShapeDtypeStruct((rows, features), out_type)],
             [pattern_two.reshape(1, slots), count_two],
             [*pieces, blocks_two.reshape(slots, size, size)],
-            [jax.ShapeDtypeStruct((columns_two + 1, rows, size), jnp.float32)],
+            [
+                jax.ShapeDtypeStruct((units, rows // groups, size), jnp.bfloat16),
+                jax.ShapeDtypeStruct((columns_two + 1, rows, size), jnp.float32),
+            ],
             rows if out_type == jnp.bfloat16 else 0,
         )[0]
 
     theirs = [across(activations, k) for k in range(1, n_cols)]
     theirs = theirs[0] if n_cols == 2 else jnp.concatenate(theirs, axis=0)
-    send, keep, stored = first(activations, None)
-    own = (send, keep)
+    *own, stored = first(activations, None)
     theirs = first(theirs, stored)
     chunks = {"theirs": theirs, "own": own}
     stages = {

time: 75.3 us -> 74.4 us (0.988)
  starting transfers between devices: 29.8 us -> 28.7 us
    ppermute x2, waiting for transfers between devices: 3.93 us -> 4.81 us  [across(): lax.ppermute(value, 'col', [(b, (b + by) % n_cols) for b in range(n_cols)])]
    ppermute x22 -> x24, starting transfers between devices: 26.2 us -> 25.4 us  [move(): return lax.ppermute(value, 'row', digit_shift(sizes, which, by))]
    ppermute x22 -> x24, waiting for transfers between devices: 32 us -> 31.7 us  [move(): return lax.ppermute(value, 'row', digit_shift(sizes, which, by))]
  transfers between devices with their start and end apart: 24 -> 26, of which waited for: 13 -> 12; matrix products, arithmetic and copies ran while one was open for 0% -> 0% of each run, Pallas kernels for 7% -> 7%
where the time goes in v1:
time: 74.4 us; the launch traced here: 74.3 us
  waiting for transfers between devices  36.5 us (49%)
  starting transfers between devices  28.7 us (39%)
  Pallas kernels  6.28 us (8%)
  between operations  1.47 us (2%)
    ppermute x24, waiting for transfers between devices, move(): return lax.ppermute(value, 'row', digit_shift(sizes, which, by))  31.7 us
    ppermute x24, starting transfers between devices, move(): return lax.ppermute(value, 'row', digit_shift(sizes, which, by))  25.4 us
    pallas_call x12, Pallas kernels, call(): pl.pallas_call(kernel, out_shape=tuple(outs), in_specs=[smem] * len(scala...  6.28 us
    ppermute x2, waiting for transfers between devices, across(): lax.ppermute(value, 'col', [(b, (b + by) % n_cols) for b in range(n_cols)])  4.81 us
    ppermute x2, starting transfers between devices, across(): lax.ppermute(value, 'col', [(b, (b + by) % n_cols) for b in range(n_cols)])  3.3 us
  transfers between devices with their start and end apart: 26, of which 12 were waited for; matrix products, arithmetic and copies ran while one was open for 0% of the time, Pallas kernels for 7%

profile of v1, /device:TPU:0, one launch (start us, length us, event | category | flops | bytes accessed | tf_op | source)
XLA Modules:
  0.0 74.3 jit_solution(13949006730733661413)
XLA Ops:
  0.0 3.0 %collective-permute-start.12 = (bf16[64,1024]{1,0:T(8,128)(2,1)}, bf16[64,1024]{1,0:T(8,128)(2,1)S(1)}, u32[]{:S(2)}, u32[]{:S(2)}) collective-permute-start(bf16[64,1024]{1,0:T(8,128)(2,1)} %act.1), channel_id=1, source_target_pairs={{0,1},{1,0},{2,3},{3,2},{4,5},{5,4},{6,7},{7,6},{8,9},{9,8},{10,11... | collective-permute-start | bytes 393224 | tf_op jit(solution)/shard_map/ppermute | solution.py:217
  3.7 0.6 copy-done.2
  4.3 2.8 %shard_map.73 = (f32[16,64,128]{2,1,0:T(8,128)S(1)}, f32[16,64,128]{2,1,0:T(8,128)S(1)}, f32[16,64,128]{2,1,0:T(8,128)S(1)}, f32[16,64,128]{2,1,0:T(8,128)S(1)}, bf16[64,128,128]{2,1,0:T(8,128)(2,1)S(1)}) custom-call(s32[1,64]{1,0:T(1,128)S(1)} %bitcast.20, s32[1,1]{1,0:T(1,128)S(6)} %copy.8.count, bf16[64,1024]{1,0:T(8,128)(2,1)} %act.1, ...), custom_call_target="tpu_custom_call" | custom-call | flops 134217728 | bytes 2097152 | tf_op jit(solution)/shard_map/pallas_call | solution.py:226
  7.1 1.2 %shard_map.79 = (f32[16,64,128]{2,1,0:T(8,128)S(1)}, f32[16,64,128]{2,1,0:T(8,128)S(1)}, f32[16,64,128]{2,1,0:T(8,128)S(1)}, f32[16,64,128]{2,1,0:T(8,128)S(1)}) custom-call(s32[1,64]{1,0:T(1,128)S(1)} %bitcast.21, s32[1,1]{1,0:T(1,128)S(6)} %copy.8.count, bf16[64,1024]{1,0:T(8,128)(2,1)S(1)} %collective-permute-done.12.act, ...), custom_call_target="tpu_custom_call" | custom-call | flops 134217728 | bytes 2097152 | tf_op jit(solution)/shard_map/pallas_call | solution.py:226
  9.4 0.9 %collective-permute-done.14.right = f32[16,64,128]{2,1,0:T(8,128)S(1)} collective-permute-done((f32[16,64,128]{2,1,0:T(8,128)S(1)}, f32[16,64,128]{2,1,0:T(8,128)S(1)}, u32[]{:S(2)}, u32[]{:S(2)}) %collective-permute-start.14) | collective-permute-done | bytes 524320 | tf_op jit(solution)/shard_map/ppermute | solution.py:214
  10.4 2.1 %collective-permute-start.15 = (bf16[16,64,128]{2,1,0:T(8,128)(2,1)S(1)}, bf16[16,64,128]{2,1,0:T(8,128)(2,1)S(1)}, u32[]{:S(2)}, u32[]{:S(2)}) collective-permute-start(bf16[16,64,128]{2,1,0:T(8,128)(2,1)S(1)} %shard_map.80), channel_id=1, source_target_pairs={{0,4},{2,6},{4,0},{6,2},{8,12},{10,14},{12,8},{14,10},{16,20},{18,... | collective-permute-start | bytes 786440 | tf_op jit(solution)/shard_map/ppermute | solution.py:214
  12.6 0.7 collective-permute-start.2
  13.3 6.4 %collective-permute-done.15 = bf16[16,64,128]{2,1,0:T(8,128)(2,1)S(1)} collective-permute-done((bf16[16,64,128]{2,1,0:T(8,128)(2,1)S(1)}, bf16[16,64,128]{2,1,0:T(8,128)(2,1)S(1)}, u32[]{:S(2)}, u32[]{:S(2)}) %collective-permute-start.15) | collective-permute-done | bytes 262176 | tf_op jit(solution)/shard_map/ppermute | solution.py:214
  19.7 2.2 %collective-permute-start.16 = (bf16[4,64,128]{2,1,0:T(8,128)(2,1)S(1)}, bf16[4,64,128]{2,1,0:T(8,128)(2,1)S(1)}, u32[]{:S(2)}, u32[]{:S(2)}) collective-permute-start(bf16[4,64,128]{2,1,0:T(8,128)(2,1)S(1)} %get-tuple-element.36), channel_id=1, source_target_pairs={{0,8},{2,10},{4,12},{6,14},{8,0},{10,2},{12,4},{14,6},{16,24},{18,... | collective-permute-start | bytes 196616 | tf_op jit(solution)/shard_map/ppermute | solution.py:214
  21.9 2.6 %collective-permute-start.17 = (bf16[4,64,128]{2,1,0:T(8,128)(2,1)S(1)}, bf16[4,64,128]{2,1,0:T(8,128)(2,1)S(1)}, u32[]{:S(2)}, u32[]{:S(2)}) collective-permute-start(bf16[4,64,128]{2,1,0:T(8,128)(2,1)S(1)} %get-tuple-element.37), channel_id=1, source_target_pairs={{0,16},{2,18},{4,20},{6,22},{8,24},{10,26},{12,28},{14,30},{16,0},... | collective-permute-start | bytes 196616 | tf_op jit(solution)/shard_map/ppermute | solution.py:214
  25.0 2.1 %collective-permute-done.17.refs_2_ = bf16[4,64,128]{2,1,0:T(8,128)(2,1)S(1)} collective-permute-done((bf16[4,64,128]{2,1,0:T(8,128)(2,1)S(1)}, bf16[4,64,128]{2,1,0:T(8,128)(2,1)S(1)}, u32[]{:S(2)}, u32[]{:S(2)}) %collective-permute-start.17) | collective-permute-done | bytes 65568 | tf_op jit(solution)/shard_map/ppermute | solution.py:214
  27.1 3.9 %collective-permute-done.18.refs_3_ = bf16[4,64,128]{2,1,0:T(8,128)(2,1)S(1)} collective-permute-done((bf16[4,64,128]{2,1,0:T(8,128)(2,1)S(1)}, bf16[4,64,128]{2,1,0:T(8,128)(2,1)S(1)}, u32[]{:S(2)}, u32[]{:S(2)}) %collective-permute-start.18) | collective-permute-done | bytes 65568 | tf_op jit(solution)/shard_map/ppermute | solution.py:214
  31.1 1.1 %collective-permute-start.20 = (bf16[4,64,128]{2,1,0:T(8,128)(2,1)S(1)}, bf16[4,64,128]{2,1,0:T(8,128)(2,1)S(1)}, u32[]{:S(2)}, u32[]{:S(2)}) collective-permute-start(bf16[4,64,128]{2,1,0:T(8,128)(2,1)S(1)} %shard_map.82.refs_0_), channel_id=1, source_target_pairs={{0,16},{2,18},{4,20},{6,22},{8,24},{10,26},{12,28},{14,30},{16,0},... | collective-permute-start | bytes 196616 | tf_op jit(solution)/shard_map/ppermute | solution.py:214
  32.2 3.3 %collective-permute-start.21 = (bf16[4,64,128]{2,1,0:T(8,128)(2,1)S(1)}, bf16[4,64,128]{2,1,0:T(8,128)(2,1)S(1)}, u32[]{:S(2)}, u32[]{:S(2)}) collective-permute-start(bf16[4,64,128]{2,1,0:T(8,128)(2,1)S(1)} %shard_map.82.refs_0_), channel_id=1, source_target_pairs={{0,24},{2,26},{4,28},{6,30},{8,16},{10,18},{12,20},{14,22},{16,8},... | collective-permute-start | bytes 196616 | tf_op jit(solution)/shard_map/ppermute | solution.py:214
  35.5 0.9 %collective-permute-done.20.refs_2_ = bf16[4,64,128]{2,1,0:T(8,128)(2,1)S(1)} collective-permute-done((bf16[4,64,128]{2,1,0:T(8,128)(2,1)S(1)}, bf16[4,64,128]{2,1,0:T(8,128)(2,1)S(1)}, u32[]{:S(2)}, u32[]{:S(2)}) %collective-permute-start.20) | collective-permute-done | bytes 65568 | tf_op jit(solution)/shard_map/ppermute | solution.py:214
  36.3 2.2 %collective-permute-done.21.refs_3_ = bf16[4,64,128]{2,1,0:T(8,128)(2,1)S(1)} collective-permute-done((bf16[4,64,128]{2,1,0:T(8,128)(2,1)S(1)}, bf16[4,64,128]{2,1,0:T(8,128)(2,1)S(1)}, u32[]{:S(2)}, u32[]{:S(2)}) %collective-permute-start.21) | collective-permute-done | bytes 65568 | tf_op jit(solution)/shard_map/ppermute | solution.py:214
  38.6 2.2 %collective-permute-start.22 = (bf16[16,64,128]{2,1,0:T(8,128)(2,1)S(1)}, bf16[16,64,128]{2,1,0:T(8,128)(2,1)S(1)}, u32[]{:S(2)}, u32[]{:S(2)}) collective-permute-start(bf16[16,64,128]{2,1,0:T(8,128)(2,1)S(1)} %shard_map.83.refs_0_), channel_id=1, source_target_pairs={{0,4},{2,6},{4,0},{6,2},{8,12},{10,14},{12,8},{14,10},{16,20},{18,... | collective-permute-start | bytes 786440 | tf_op jit(solution)/shard_map/ppermute | solution.py:214
  40.9 3.7 %collective-permute-start.4 = (bf16[4,64,128]{2,1,0:T(8,128)(2,1)S(1)}, bf16[4,64,128]{2,1,0:T(8,128)(2,1)S(1)}, u32[]{:S(2)}, u32[]{:S(2)}) collective-permute-start(bf16[4,64,128]{2,1,0:T(8,128)(2,1)S(1)} %get-tuple-element.28), channel_id=1, source_target_pairs={{0,16},{2,18},{4,20},{6,22},{8,24},{10,26},{12,28},{14,30},{16,0},... | collective-permute-start | bytes 196616 | tf_op jit(solution)/shard_map/ppermute | solution.py:214
  44.6 0.7 collective-permute-start.5
  45.3 1.7 %collective-permute-done.4.refs_2_ = bf16[4,64,128]{2,1,0:T(8,128)(2,1)S(1)} collective-permute-done((bf16[4,64,128]{2,1,0:T(8,128)(2,1)S(1)}, bf16[4,64,128]{2,1,0:T(8,128)(2,1)S(1)}, u32[]{:S(2)}, u32[]{:S(2)}) %collective-permute-start.4) | collective-permute-done | bytes 65568 | tf_op jit(solution)/shard_map/ppermute | solution.py:214
  47.0 3.7 %collective-permute-done.5.refs_3_ = bf16[4,64,128]{2,1,0:T(8,128)(2,1)S(1)} collective-permute-done((bf16[4,64,128]{2,1,0:T(8,128)(2,1)S(1)}, bf16[4,64,128]{2,1,0:T(8,128)(2,1)S(1)}, u32[]{:S(2)}, u32[]{:S(2)}) %collective-permute-start.5) | collective-permute-done | bytes 65568 | tf_op jit(solution)/shard_map/ppermute | solution.py:214
  50.8 1.3 %collective-permute-start.6 = (bf16[4,64,128]{2,1,0:T(8,128)(2,1)S(1)}, bf16[4,64,128]{2,1,0:T(8,128)(2,1)S(1)}, u32[]{:S(2)}, u32[]{:S(2)}) collective-permute-start(bf16[4,64,128]{2,1,0:T(8,128)(2,1)S(1)} %shard_map.76.refs_0_), channel_id=1, source_target_pairs={{0,8},{2,10},{4,12},{6,14},{8,0},{10,2},{12,4},{14,6},{16,24},{18,... | collective-permute-start | bytes 196616 | tf_op jit(solution)/shard_map/ppermute | solution.py:214
  52.0 1.2 %collective-permute-start.7 = (bf16[4,64,128]{2,1,0:T(8,128)(2,1)S(1)}, bf16[4,64,128]{2,1,0:T(8,128)(2,1)S(1)}, u32[]{:S(2)}, u32[]{:S(2)}) collective-permute-start(bf16[4,64,128]{2,1,0:T(8,128)(2,1)S(1)} %shard_map.76.refs_0_), channel_id=1, source_target_pairs={{0,16},{2,18},{4,20},{6,22},{8,24},{10,26},{12,28},{14,30},{16,0},... | collective-permute-start | bytes 196616 | tf_op jit(solution)/shard_map/ppermute | solution.py:214
  53.2 2.0 %collective-permute-start.8 = (bf16[4,64,128]{2,1,0:T(8,128)(2,1)S(1)}, bf16[4,64,128]{2,1,0:T(8,128)(2,1)S(1)}, u32[]{:S(2)}, u32[]{:S(2)}) collective-permute-start(bf16[4,64,128]{2,1,0:T(8,128)(2,1)S(1)} %shard_map.76.refs_0_), channel_id=1, source_target_pairs={{0,24},{2,26},{4,28},{6,30},{8,16},{10,18},{12,20},{14,22},{16,8},... | collective-permute-start | bytes 196616 | tf_op jit(solution)/shard_map/ppermute | solution.py:214
  55.2 2.7 %collective-permute-done.7.refs_2_ = bf16[4,64,128]{2,1,0:T(8,128)(2,1)S(1)} collective-permute-done((bf16[4,64,128]{2,1,0:T(8,128)(2,1)S(1)}, bf16[4,64,128]{2,1,0:T(8,128)(2,1)S(1)}, u32[]{:S(2)}, u32[]{:S(2)}) %collective-permute-start.7) | collective-permute-done | bytes 65568 | tf_op jit(solution)/shard_map/ppermute | solution.py:214
  57.9 1.5 %collective-permute-done.8.refs_3_ = bf16[4,64,128]{2,1,0:T(8,128)(2,1)S(1)} collective-permute-done((bf16[4,64,128]{2,1,0:T(8,128)(2,1)S(1)}, bf16[4,64,128]{2,1,0:T(8,128)(2,1)S(1)}, u32[]{:S(2)}, u32[]{:S(2)}) %collective-permute-start.8) | collective-permute-done | bytes 65568 | tf_op jit(solution)/shard_map/ppermute | solution.py:214
  59.6 0.5 collective-permute-start.24
  60.2 5.7 %collective-permute-done.9.refs_1_ = bf16[16,64,128]{2,1,0:T(8,128)(2,1)S(1)} collective-permute-done((bf16[16,64,128]{2,1,0:T(8,128)(2,1)S(1)}, bf16[16,64,128]{2,1,0:T(8,128)(2,1)S(1)}, u32[]{:S(2)}, u32[]{:S(2)}) %collective-permute-start.9) | collective-permute-done | bytes 262176 | tf_op jit(solution)/shard_map/ppermute | solution.py:214
  66.5 0.9 %shard_map.84 = bf16[64,1024]{1,0:T(8,128)(2,1)S(1)} custom-call(s32[1,64]{1,0:T(1,128)S(1)} %bitcast.18, s32[1,1]{1,0:T(1,128)S(6)} %copy.9.count, bf16[16,64,128]{2,1,0:T(8,128)(2,1)S(1)} %shard_map.83.refs_0_, bf16[16,64,128]{2,1,0:T(8,128)(2,1)S(1)} %collective-permute-done.22.refs_1_, bf16[16,64,128]{2,1,0:T(8,128)(2,1)S(1)} %collective-permute-done.23.refs_2_, ...), custom_call_target="tpu_custom_call" | custom-call | flops 134217728 | bytes 2097152 | tf_op jit(solution)/shard_map/pallas_call | solution.py:226
  67.8 0.9 %shard_map.78 = f32[64,1024]{1,0:T(8,128)S(1)} custom-call(s32[1,64]{1,0:T(1,128)S(1)} %bitcast.19, s32[1,1]{1,0:T(1,128)S(6)} %copy.9.count, bf16[16,64,128]{2,1,0:T(8,128)(2,1)S(1)} %shard_map.77.refs_0_, bf16[16,64,128]{2,1,0:T(8,128)(2,1)S(1)} %collective-permute-done.9.refs_1_, bf16[16,64,128]{2,1,0:T(8,128)(2,1)S(1)} %collective-permute-done.10.refs_2_, ...), custom_call_target="tpu_custom_call" | custom-call | tf_op jit(solution)/shard_map/pallas_call | solution.py:226
  68.8 4.8 %collective-permute-done.25 = bf16[64,1024]{1,0:T(8,128)(2,1)S(1)} collective-permute-done((bf16[64,1024]{1,0:T(8,128)(2,1)S(1)}, bf16[64,1024]{1,0:T(8,128)(2,1)S(1)}, u32[]{:S(2)}, u32[]{:S(2)}) %collective-permute-start.25) | collective-permute-done | bytes 131104 | tf_op jit(solution)/shard_map/ppermute | solution.py:217
  73.6 0.7 maximum_convert_fusion
  (39 shorter events, 2.6 us)
Async XLA Ops:
  0.0 7.1 %collective-permute-start.12 = (bf16[64,1024]{1,0:T(8,128)(2,1)}, bf16[64,1024]{1,0:T(8,128)(2,1)S(1)}, u32[]{:S(2)}, u32[]{:S(2)}) collective-permute-start(bf16[64,1024]{1,0:T(8,128)(2,1)} %act.1), channel_id=1, source_target_pairs={{0,1},{1,0},{2,3},{3,2},{4,5},{5,4},{6,7},{7,6},{8,9},{9,8},{10,11... | collective-permute-start | bytes 393224 | tf_op jit(solution)/shard_map/ppermute | solution.py:217
  3.6 0.7 copy-start.2
  8.3 2.0 %collective-permute-start.14 = (f32[16,64,128]{2,1,0:T(8,128)S(1)}, f32[16,64,128]{2,1,0:T(8,128)S(1)}, u32[]{:S(2)}, u32[]{:S(2)}) collective-permute-start(f32[16,64,128]{2,1,0:T(8,128)S(1)} %get-tuple-element.34), channel_id=1, source_target_pairs={{0,2},{2,0},{4,6},{6,4},{8,10},{10,8},{12,14},{14,12},{16,18},{18,... | collective-permute-start | bytes 1572872 | tf_op jit(solution)/shard_map/ppermute | solution.py:214
  8.4 4.1 %collective-permute-start.1 = (f32[16,64,128]{2,1,0:T(8,128)S(1)}, f32[16,64,128]{2,1,0:T(8,128)S(1)}, u32[]{:S(2)}, u32[]{:S(2)}) collective-permute-start(f32[16,64,128]{2,1,0:T(8,128)S(1)} %get-tuple-element.25), channel_id=1, source_target_pairs={{0,2},{2,0},{4,6},{6,4},{8,10},{10,8},{12,14},{14,12},{16,18},{18,... | collective-permute-start | bytes 1572872 | tf_op jit(solution)/shard_map/ppermute | solution.py:214
  8.9 4.3 %collective-permute-start.13 = (f32[16,64,128]{2,1,0:T(8,128)S(1)}, f32[16,64,128]{2,1,0:T(8,128)S(1)}, u32[]{:S(2)}, u32[]{:S(2)}) collective-permute-start(f32[16,64,128]{2,1,0:T(8,128)S(1)} %get-tuple-element.32), channel_id=1, source_target_pairs={{0,2},{2,0},{4,6},{6,4},{8,10},{10,8},{12,14},{14,12},{16,18},{18,... | collective-permute-start | bytes 1572872 | tf_op jit(solution)/shard_map/ppermute | solution.py:214
  9.0 31.8 %collective-permute-start = (f32[16,64,128]{2,1,0:T(8,128)S(1)}, f32[16,64,128]{2,1,0:T(8,128)S(1)}, u32[]{:S(2)}, u32[]{:S(2)}) collective-permute-start(f32[16,64,128]{2,1,0:T(8,128)S(1)} %get-tuple-element.23), channel_id=1, source_target_pairs={{0,2},{2,0},{4,6},{6,4},{8,10},{10,8},{12,14},{14,12},{16,18},{18,... | collective-permute-start | bytes 1572872 | tf_op jit(solution)/shard_map/ppermute | solution.py:214
  10.4 9.3 %collective-permute-start.15 = (bf16[16,64,128]{2,1,0:T(8,128)(2,1)S(1)}, bf16[16,64,128]{2,1,0:T(8,128)(2,1)S(1)}, u32[]{:S(2)}, u32[]{:S(2)}) collective-permute-start(bf16[16,64,128]{2,1,0:T(8,128)(2,1)S(1)} %shard_map.80), channel_id=1, source_target_pairs={{0,4},{2,6},{4,0},{6,2},{8,12},{10,14},{12,8},{14,10},{16,20},{18,... | collective-permute-start | bytes 786440 | tf_op jit(solution)/shard_map/ppermute | solution.py:214
  12.6 28.2 %collective-permute-start.2 = (bf16[16,64,128]{2,1,0:T(8,128)(2,1)S(1)}, bf16[16,64,128]{2,1,0:T(8,128)(2,1)S(1)}, u32[]{:S(2)}, u32[]{:S(2)}) collective-permute-start(bf16[16,64,128]{2,1,0:T(8,128)(2,1)S(1)} %shard_map.74), channel_id=1, source_target_pairs={{0,4},{2,6},{4,0},{6,2},{8,12},{10,14},{12,8},{14,10},{16,20},{18,... | collective-permute-start | bytes 786440 | tf_op jit(solution)/shard_map/ppermute | solution.py:214
  19.7 46.9 %copy-start = (bf16[1,1,64,128,128]{4,3,2,1,0:T(8,128)(2,1)S(1)}, bf16[1,1,64,128,128]{4,3,2,1,0:T(8,128)(2,1)}, u32[]{:S(2)}) copy-start(bf16[1,1,64,128,128]{4,3,2,1,0:T(8,128)(2,1)} %param.11) | copy-start | bytes 6291460
  19.7 46.9 %copy-start.1 = (s32[1,1,64]{2,1,0:T(1,128)S(1)}, s32[1,1,64]{2,1,0:T(1,128)}, u32[]{:S(2)}) copy-start(s32[1,1,64]{2,1,0:T(1,128)} %param.12) | copy-start | bytes 772
  19.7 5.2 %collective-permute-start.16 = (bf16[4,64,128]{2,1,0:T(8,128)(2,1)S(1)}, bf16[4,64,128]{2,1,0:T(8,128)(2,1)S(1)}, u32[]{:S(2)}, u32[]{:S(2)}) collective-permute-start(bf16[4,64,128]{2,1,0:T(8,128)(2,1)S(1)} %get-tuple-element.36), channel_id=1, source_target_pairs={{0,8},{2,10},{4,12},{6,14},{8,0},{10,2},{12,4},{14,6},{16,24},{18,... | collective-permute-start | bytes 196616 | tf_op jit(solution)/shard_map/ppermute | solution.py:214
  21.9 5.2 %collective-permute-start.17 = (bf16[4,64,128]{2,1,0:T(8,128)(2,1)S(1)}, bf16[4,64,128]{2,1,0:T(8,128)(2,1)S(1)}, u32[]{:S(2)}, u32[]{:S(2)}) collective-permute-start(bf16[4,64,128]{2,1,0:T(8,128)(2,1)S(1)} %get-tuple-element.37), channel_id=1, source_target_pairs={{0,16},{2,18},{4,20},{6,22},{8,24},{10,26},{12,28},{14,30},{16,0},... | collective-permute-start | bytes 196616 | tf_op jit(solution)/shard_map/ppermute | solution.py:214
  24.5 6.4 %collective-permute-start.18 = (bf16[4,64,128]{2,1,0:T(8,128)(2,1)S(1)}, bf16[4,64,128]{2,1,0:T(8,128)(2,1)S(1)}, u32[]{:S(2)}, u32[]{:S(2)}) collective-permute-start(bf16[4,64,128]{2,1,0:T(8,128)(2,1)S(1)} %get-tuple-element.38), channel_id=1, source_target_pairs={{0,24},{2,26},{4,28},{6,30},{8,16},{10,18},{12,20},{14,22},{16,8},... | collective-permute-start | bytes 196616 | tf_op jit(solution)/shard_map/ppermute | solution.py:214
  31.0 4.5 %collective-permute-start.19 = (bf16[4,64,128]{2,1,0:T(8,128)(2,1)S(1)}, bf16[4,64,128]{2,1,0:T(8,128)(2,1)S(1)}, u32[]{:S(2)}, u32[]{:S(2)}) collective-permute-start(bf16[4,64,128]{2,1,0:T(8,128)(2,1)S(1)} %shard_map.82.refs_0_), channel_id=1, source_target_pairs={{0,8},{2,10},{4,12},{6,14},{8,0},{10,2},{12,4},{14,6},{16,24},{18,... | collective-permute-start | bytes 196616 | tf_op jit(solution)/shard_map/ppermute | solution.py:214
  31.1 5.2 %collective-permute-start.20 = (bf16[4,64,128]{2,1,0:T(8,128)(2,1)S(1)}, bf16[4,64,128]{2,1,0:T(8,128)(2,1)S(1)}, u32[]{:S(2)}, u32[]{:S(2)}) collective-permute-start(bf16[4,64,128]{2,1,0:T(8,128)(2,1)S(1)} %shard_map.82.refs_0_), channel_id=1, source_target_pairs={{0,16},{2,18},{4,20},{6,22},{8,24},{10,26},{12,28},{14,30},{16,0},... | collective-permute-start | bytes 196616 | tf_op jit(solution)/shard_map/ppermute | solution.py:214
  32.2 6.3 %collective-permute-start.21 = (bf16[4,64,128]{2,1,0:T(8,128)(2,1)S(1)}, bf16[4,64,128]{2,1,0:T(8,128)(2,1)S(1)}, u32[]{:S(2)}, u32[]{:S(2)}) collective-permute-start(bf16[4,64,128]{2,1,0:T(8,128)(2,1)S(1)} %shard_map.82.refs_0_), channel_id=1, source_target_pairs={{0,24},{2,26},{4,28},{6,30},{8,16},{10,18},{12,20},{14,22},{16,8},... | collective-permute-start | bytes 196616 | tf_op jit(solution)/shard_map/ppermute | solution.py:214
  38.6 21.1 %collective-permute-start.22 = (bf16[16,64,128]{2,1,0:T(8,128)(2,1)S(1)}, bf16[16,64,128]{2,1,0:T(8,128)(2,1)S(1)}, u32[]{:S(2)}, u32[]{:S(2)}) collective-permute-start(bf16[16,64,128]{2,1,0:T(8,128)(2,1)S(1)} %shard_map.83.refs_0_), channel_id=1, source_target_pairs={{0,4},{2,6},{4,0},{6,2},{8,12},{10,14},{12,8},{14,10},{16,20},{18,... | collective-permute-start | bytes 786440 | tf_op jit(solution)/shard_map/ppermute | solution.py:214
  40.9 4.5 %collective-permute-start.3 = (bf16[4,64,128]{2,1,0:T(8,128)(2,1)S(1)}, bf16[4,64,128]{2,1,0:T(8,128)(2,1)S(1)}, u32[]{:S(2)}, u32[]{:S(2)}) collective-permute-start(bf16[4,64,128]{2,1,0:T(8,128)(2,1)S(1)} %get-tuple-element.27), channel_id=1, source_target_pairs={{0,8},{2,10},{4,12},{6,14},{8,0},{10,2},{12,4},{14,6},{16,24},{18,... | collective-permute-start | bytes 196616 | tf_op jit(solution)/shard_map/ppermute | solution.py:214
  40.9 6.0 %collective-permute-start.4 = (bf16[4,64,128]{2,1,0:T(8,128)(2,1)S(1)}, bf16[4,64,128]{2,1,0:T(8,128)(2,1)S(1)}, u32[]{:S(2)}, u32[]{:S(2)}) collective-permute-start(bf16[4,64,128]{2,1,0:T(8,128)(2,1)S(1)} %get-tuple-element.28), channel_id=1, source_target_pairs={{0,16},{2,18},{4,20},{6,22},{8,24},{10,26},{12,28},{14,30},{16,0},... | collective-permute-start | bytes 196616 | tf_op jit(solution)/shard_map/ppermute | solution.py:214
  44.6 6.1 %collective-permute-start.5 = (bf16[4,64,128]{2,1,0:T(8,128)(2,1)S(1)}, bf16[4,64,128]{2,1,0:T(8,128)(2,1)S(1)}, u32[]{:S(2)}, u32[]{:S(2)}) collective-permute-start(bf16[4,64,128]{2,1,0:T(8,128)(2,1)S(1)} %get-tuple-element.29), channel_id=1, source_target_pairs={{0,24},{2,26},{4,28},{6,30},{8,16},{10,18},{12,20},{14,22},{16,8},... | collective-permute-start | bytes 196616 | tf_op jit(solution)/shard_map/ppermute | solution.py:214
  50.8 4.5 %collective-permute-start.6 = (bf16[4,64,128]{2,1,0:T(8,128)(2,1)S(1)}, bf16[4,64,128]{2,1,0:T(8,128)(2,1)S(1)}, u32[]{:S(2)}, u32[]{:S(2)}) collective-permute-start(bf16[4,64,128]{2,1,0:T(8,128)(2,1)S(1)} %shard_map.76.refs_0_), channel_id=1, source_target_pairs={{0,8},{2,10},{4,12},{6,14},{8,0},{10,2},{12,4},{14,6},{16,24},{18,... | collective-permute-start | bytes 196616 | tf_op jit(solution)/shard_map/ppermute | solution.py:214
  52.0 5.9 %collective-permute-start.7 = (bf16[4,64,128]{2,1,0:T(8,128)(2,1)S(1)}, bf16[4,64,128]{2,1,0:T(8,128)(2,1)S(1)}, u32[]{:S(2)}, u32[]{:S(2)}) collective-permute-start(bf16[4,64,128]{2,1,0:T(8,128)(2,1)S(1)} %shard_map.76.refs_0_), channel_id=1, source_target_pairs={{0,16},{2,18},{4,20},{6,22},{8,24},{10,26},{12,28},{14,30},{16,0},... | collective-permute-start | bytes 196616 | tf_op jit(solution)/shard_map/ppermute | solution.py:214
  53.2 6.2 %collective-permute-start.8 = (bf16[4,64,128]{2,1,0:T(8,128)(2,1)S(1)}, bf16[4,64,128]{2,1,0:T(8,128)(2,1)S(1)}, u32[]{:S(2)}, u32[]{:S(2)}) collective-permute-start(bf16[4,64,128]{2,1,0:T(8,128)(2,1)S(1)} %shard_map.76.refs_0_), channel_id=1, source_target_pairs={{0,24},{2,26},{4,28},{6,30},{8,16},{10,18},{12,20},{14,22},{16,8},... | collective-permute-start | bytes 196616 | tf_op jit(solution)/shard_map/ppermute | solution.py:214
  59.4 6.4 %collective-permute-start.9 = (bf16[16,64,128]{2,1,0:T(8,128)(2,1)S(1)}, bf16[16,64,128]{2,1,0:T(8,128)(2,1)S(1)}, u32[]{:S(2)}, u32[]{:S(2)}) collective-permute-start(bf16[16,64,128]{2,1,0:T(8,128)(2,1)S(1)} %shard_map.77.refs_0_), channel_id=1, source_target_pairs={{0,4},{2,6},{4,0},{6,2},{8,12},{10,14},{12,8},{14,10},{16,20},{18,... | collective-permute-start | bytes 786440 | tf_op jit(solution)/shard_map/ppermute | solution.py:214
  59.6 6.9 %collective-permute-start.23 = (bf16[16,64,128]{2,1,0:T(8,128)(2,1)S(1)}, bf16[16,64,128]{2,1,0:T(8,128)(2,1)S(1)}, u32[]{:S(2)}, u32[]{:S(2)}) collective-permute-start(bf16[16,64,128]{2,1,0:T(8,128)(2,1)S(1)} %shard_map.83.refs_0_), channel_id=1, source_target_pairs={{0,2},{2,0},{4,6},{6,4},{8,10},{10,8},{12,14},{14,12},{16,18},{18,... | collective-permute-start | bytes 786440 | tf_op jit(solution)/shard_map/ppermute | solution.py:214
  59.6 6.9 %collective-permute-start.24 = (bf16[16,64,128]{2,1,0:T(8,128)(2,1)S(1)}, bf16[16,64,128]{2,1,0:T(8,128)(2,1)S(1)}, u32[]{:S(2)}, u32[]{:S(2)}) collective-permute-start(bf16[16,64,128]{2,1,0:T(8,128)(2,1)S(1)} %collective-permute-done.22.refs_1_), channel_id=1, source_target_pairs={{0,2},{2,0},{4,6},{6,4},{8,10},{10,8},{12,14},{14,12},{16,18},{18,... | collective-permute-start | bytes 786440 | tf_op jit(solution)/shard_map/ppermute | solution.py:214
  60.2 7.6 %collective-permute-start.10 = (bf16[16,64,128]{2,1,0:T(8,128)(2,1)S(1)}, bf16[16,64,128]{2,1,0:T(8,128)(2,1)S(1)}, u32[]{:S(2)}, u32[]{:S(2)}) collective-permute-start(bf16[16,64,128]{2,1,0:T(8,128)(2,1)S(1)} %shard_map.77.refs_0_), channel_id=1, source_target_pairs={{0,2},{2,0},{4,6},{6,4},{8,10},{10,8},{12,14},{14,12},{16,18},{18,... | collective-permute-start | bytes 786440 | tf_op jit(solution)/shard_map/ppermute | solution.py:214
  65.8 2.0 %collective-permute-start.11 = (bf16[16,64,128]{2,1,0:T(8,128)(2,1)S(1)}, bf16[16,64,128]{2,1,0:T(8,128)(2,1)S(1)}, u32[]{:S(2)}, u32[]{:S(2)}) collective-permute-start(bf16[16,64,128]{2,1,0:T(8,128)(2,1)S(1)} %collective-permute-done.9.refs_1_), channel_id=1, source_target_pairs={{0,2},{2,0},{4,6},{6,4},{8,10},{10,8},{12,14},{14,12},{16,18},{18,... | collective-permute-start | bytes 786440 | tf_op jit(solution)/shard_map/ppermute | solution.py:214
  67.5 6.1 %collective-permute-start.25 = (bf16[64,1024]{1,0:T(8,128)(2,1)S(1)}, bf16[64,1024]{1,0:T(8,128)(2,1)S(1)}, u32[]{:S(2)}, u32[]{:S(2)}) collective-permute-start(bf16[64,1024]{1,0:T(8,128)(2,1)S(1)} %shard_map.84), channel_id=1, source_target_pairs={{0,1},{1,0},{2,3},{3,2},{4,5},{5,4},{6,7},{7,6},{8,9},{9,8},{10,11... | collective-permute-start | bytes 393224 | tf_op jit(solution)/shard_map/ppermute | solution.py:217
